TPU v7x, 256 devices: a whole 4x4x8 slice. The times are simulated.
256 devices in a mesh: ep: 128 (over z, x, y), half: 2 (over core).
Axes of the slice: x: 4, y: 4, z: 8, core: 2. Of those that a mesh axis runs over, the one named last changes fastest.
Arguments:
- tokens: bfloat16 [16384, 2048], P('ep', 'half'), may hold values from -6 to 6
- gate_weights: float32 [16384, 8], P('ep'), may hold values from 0.05 to 0.3
- expert_ids: int32 [16384, 8], P('ep'), may hold values from 0 to 127, all different within a row; in each aligned block of 128 rows (0 to 127, 128 to 255, ...) at most 10 rows name the same one
- w_gate: bfloat16 [128, 2048, 768], P('ep', None, 'half'), may hold values from -0.125 to 0.125
- w_up: bfloat16 [128, 2048, 768], P('ep', None, 'half'), may hold values from -0.125 to 0.125
- w_down: bfloat16 [128, 768, 2048], P('ep', 'half'), may hold values from -0.21875 to 0.21875
Outputs:
- mixed: bfloat16 [16384, 2048], P('ep', 'half')
Inputs may be any that keep to these rules, and one draw needn't show every extreme that they name: `expert_ids`: each row names 8 different experts. Within the rows of one device (aligned blocks of 128 rows) no expert is named by more than 10 rows, and in every draw some expert is named by exactly 10 rows of some block.
All inputs are finite; a program needn't handle non-finite values.
Results may differ from a plain program's by a relative error of at most 0.0085.
Values may be sent and summed in bfloat16 or wider, within the bound.
A program may use at most 64 MiB of HBM per device.

v0:
```python
import jax
import jax.numpy as jnp
from jax import lax
from jax.sharding import PartitionSpec as P


def cut_along(value, dim, size):
    lengths = value.shape
    blocks = value.reshape(*lengths[:dim], size, lengths[dim] // size, *lengths[dim + 1 :])
    return jnp.moveaxis(blocks, dim, 0)


def summed_on_arrival(value, axis, dim):
    size = lax.axis_size(axis)
    blocks = lax.all_to_all(cut_along(value, dim, size), axis, 0, 0, tiled=True)
    return jnp.sum(blocks.astype(jnp.float32), axis=0)


def local(tokens, gate_weights, expert_ids, w_gate, w_up, w_down):
    tok_dev, half_width = tokens.shape
    top = expert_ids.shape[1]
    local_experts = w_gate.shape[0]
    experts = local_experts * lax.axis_size("ep")
    capacity = min(tok_dev, max(2, 5 * tok_dev * top // (4 * experts)))
    flat_ids = expert_ids.reshape(-1)
    columns = jnp.arange(experts, dtype=jnp.int32)
    onehot = (flat_ids[:, None] == columns[None, :]).astype(jnp.int32)
    ranks = jnp.sum((jnp.cumsum(onehot, axis=0) - onehot) * onehot, axis=1)
    slot = flat_ids * capacity + ranks
    token_of_pair = jnp.arange(tok_dev * top, dtype=jnp.int32) // top
    token_table = jnp.zeros((experts * capacity,), jnp.int32).at[slot].set(token_of_pair)
    filled = (
        jnp.zeros((experts * capacity,), jnp.bfloat16)
        .at[slot]
        .set(jnp.ones((tok_dev * top,), jnp.bfloat16))
    )
    outgoing = (tokens[token_table] * filled[:, None]).reshape(experts, capacity, half_width)
    received = lax.all_to_all(outgoing, "ep", split_axis=0, concat_axis=0, tiled=True)
    count = received.shape[1]
    whole = lax.all_gather(received, "half", axis=2, tiled=True)
    width = whole.shape[2]
    grouped = whole.reshape(-1, local_experts, count, width)
    gate = jnp.einsum("secd,edf->secf", grouped, w_gate, preferred_element_type=jnp.float32)
    up = jnp.einsum("secd,edf->secf", grouped, w_up, preferred_element_type=jnp.float32)
    hidden = (jax.nn.silu(gate) * up).astype(jnp.bfloat16)
    partial_out = jnp.einsum("secf,efd->secd", hidden, w_down, preferred_element_type=jnp.float32)
    partial_out = partial_out.astype(jnp.bfloat16).reshape(experts, count, width)
    widened = lax.optimization_barrier(partial_out).astype(jnp.float32)
    summed = summed_on_arrival(widened.astype(jnp.bfloat16), "half", 2).astype(jnp.bfloat16)
    answer = lax.all_to_all(summed, "ep", split_axis=0, concat_axis=0, tiled=True)
    picked = answer.reshape(experts * capacity, -1)[slot].reshape(tok_dev, top, -1)
    slot_out = picked.astype(jnp.float32)
    mixed = jnp.einsum("tk,tkx->tx", gate_weights, slot_out)
    return mixed.astype(jnp.bfloat16)


def solution(mesh):
    placed = (
        P("ep", "half"),
        P("ep", None),
        P("ep", None),
        P("ep", None, "half"),
        P("ep", None, "half"),
        P("ep", "half", None),
    )
    return jax.shard_map(
        local, mesh=mesh, in_specs=placed, out_specs=P("ep", "half"), check_vma=False
    )
```

profile of v0, /device:TPU:24, one launch (start us, length us, event | category | flops | bytes accessed | tf_op | source)
XLA Modules:
  0.0 341.7 jit_solution(1037426813920486707)
XLA Ops:
  6.5 0.9 copy.24
  7.6 0.7 broadcast_multiply_fusion.1
  8.4 0.2 fusion.17
  9.1 0.4 fusion.16
  9.4 4.3 %scatter_custom_fusion = s32[1280]{0:T(1024)S(1)} fusion(s32[1024]{0:T(1024)S(1)} %bitcast.85, s32[1024]{0:T(1024)S(1)} %add_select_fusion, s32[]{:T(128)} %constant.29.clone.1), kind=kCustom, calls=%fused_computation.41 | custom fusion | bytes 5124 | tf_op jit(solution)/shard_map/scatter | solution.py:31
  13.8 5.1 %gather_fusion = bf16[1280,1024]{1,0:T(8,128)(2,1)} fusion(bf16[128,1024]{1,0:T(8,128)(2,1)S(1)} %copy-done.1, s32[2048]{0:T(1024)S(1)} %pad_clamp_fusion), kind=kCustom, calls=%fused_computation | custom fusion | bytes 5248000 | tf_op jit(solution)/shard_map/gather | solution.py:37
  18.9 5.9 %gather.9 = bf16[128,10,1024]{2,1,0:T(8,128)(2,1)} reshape(bf16[1280,1024]{1,0:T(8,128)(2,1)} %gather_fusion) | data formatting | bytes 5242880 | tf_op jit(solution)/shard_map/gather | solution.py:37
  24.8 7.6 %scatter_custom_fusion.1 = bf16[1280]{0:T(1024)(128)(2,1)S(1)} fusion(s32[1024]{0:T(1024)S(1)} %bitcast.86, bf16[1024]{0:T(1024)(128)(2,1)S(1)} %broadcast.65, bf16[]{:T(256)} %constant.37.clone.1), kind=kCustom, calls=%fused_computation.45 | custom fusion | bytes 2562 | tf_op jit(solution)/shard_map/scatter | solution.py:35
  32.6 2.5 broadcast_multiply_fusion
  35.1 110.8 %all_to_all.15 = bf16[128,10,1024]{2,1,0:T(8,128)(2,1)S(1)} all-to-all(bf16[128,10,1024]{2,1,0:T(8,128)(2,1)S(1)} %broadcast_multiply_fusion), channel_id=1, replica_groups=mesh['ep'=128,'half'=2] {'ep'}, dimensions={0} | all-to-all | bytes 5242880 | tf_op jit(solution)/shard_map/all_to_all | solution.py:38
  145.9 2.9 copy.28
  148.9 17.1 %all-gather.2.cloned.1.call-done = bf16[128,10,2048]{2,0,1:T(8,128)(2,1)} async-done(((bf16[128,10,1024]{2,0,1:T(8,128)(2,1)}), bf16[128,10,2048]{2,0,1:T(8,128)(2,1)}) %all-gather.2.cloned.1.call-update) | async-done | bytes 5242896 | tf_op jit(solution)/shard_map/all_gather | solution.py:40
  166.0 7.1 %fusion.8 = f32[128,10,384]{2,0,1:T(8,128)} fusion(bf16[128,10,2048]{2,0,1:T(8,128)(2,1)} %all-gather.2.cloned.1.call-done, bf16[1,2048,384]{2,1,0:T(8,128)(2,1)} %param.9), kind=kOutput, calls=%fused_computation.18 | convolution fusion | flops 2013265920 | bytes 8781824 | tf_op jit(solution)/shard_map/secd,edf->secf/dot_general | solution.py:43
  173.1 9.8 %convolution_convert_fusion = bf16[128,10,2048]{2,0,1:T(8,128)(2,1)} fusion(bf16[1,384,2048]{2,1,0:T(8,128)(2,1)S(1)} %copy-done, bf16[128,10,2048]{2,0,1:T(8,128)(2,1)} %all-gather.2.cloned.1.call-done, bf16[1,2048,384]{2,1,0:T(8,128)(2,1)} %param.10, f32[128,10,384]{2,0,1:T(8,128)} %fusion.8), kind=kOutput, calls=%fused_computation.5 | convolution fusion | flops 4032102400 | bytes 15597568 | tf_op jit(solution)/shard_map/secf,efd->secd/dot_general | solution.py:46
  182.9 3.3 copy.38
  186.3 9.1 %all_to_all.16 = bf16[2,128,10,1024]{3,1,2,0:T(8,128)(2,1)} all-to-all(bf16[2,128,10,1024]{3,1,2,0:T(8,128)(2,1)S(1)} %bitcast.82), channel_id=1, replica_groups=mesh['ep'=128,'half'=2] {'half'}, dimensions={0} | all-to-all | bytes 10485760 | tf_op jit(solution)/shard_map/all_to_all | solution.py:15
  195.3 6.2 %reduce_sum.25 = bf16[128,10,1024]{2,0,1:T(8,128)(2,1)} reduce(bf16[2,128,10,1024]{3,1,2,0:T(8,128)(2,1)} %all_to_all.16, bf16[]{:T(256)} %constant.37.clone.1), dimensions={0}, to_apply=%region_5.6 | reduce | flops 1310720 | bytes 7864322 | tf_op jit(solution)/shard_map/reduce_sum | solution.py:16
  201.6 5.3 %copy.31 = bf16[128,10,1024]{2,1,0:T(8,128)(2,1)} copy(bf16[128,10,1024]{2,0,1:T(8,128)(2,1)} %reduce_sum.25) | data formatting | bytes 5242880 | tf_op jit(solution)/shard_map/reduce_sum | solution.py:16
  206.9 14.3 %all-to-all-start.2 = ((bf16[128,10,1024]{2,1,0:T(8,128)(2,1)}), bf16[128,10,1024]{2,1,0:T(8,128)(2,1)}, u32[]{:S(2)}, u32[]{:S(2)}) async-start(bf16[128,10,1024]{2,1,0:T(8,128)(2,1)} %copy.31), calls=%async_computation.2 | async-start | bytes 8388608 | tf_op jit(solution)/shard_map/all_to_all | solution.py:50
  221.4 96.1 %all-to-all-done.2 = bf16[128,10,1024]{2,1,0:T(8,128)(2,1)} async-done(((bf16[128,10,1024]{2,1,0:T(8,128)(2,1)}), bf16[128,10,1024]{2,1,0:T(8,128)(2,1)}, u32[]{:S(2)}, u32[]{:S(2)}) %all-to-all-start.2) | async-done | bytes 2621472 | tf_op jit(solution)/shard_map/all_to_all | solution.py:50
  317.5 6.1 %reshape.91 = bf16[1280,1024]{1,0:T(8,128)(2,1)} reshape(bf16[128,10,1024]{2,1,0:T(8,128)(2,1)} %all-to-all-done.2) | data formatting | bytes 5242880 | tf_op jit(solution)/shard_map/reshape | solution.py:51
  323.7 8.1 %gather_fusion.1 = bf16[1024,1024]{1,0:T(8,128)(2,1)} fusion(bf16[1280,1024]{1,0:T(8,128)(2,1)} %reshape.91, s32[1024]{0:T(1024)S(1)} %broadcast_clamp_fusion), kind=kCustom, calls=%fused_computation.1 | custom fusion | bytes 4198400 | tf_op jit(solution)/shard_map/gather | solution.py:51
  331.8 2.3 fusion
  334.1 0.8 copy.39
  (26 shorter events, 1.0 us)
Async XLA Ops:
  6.5 166.6 %copy-start = (bf16[1,384,2048]{2,1,0:T(8,128)(2,1)S(1)}, bf16[1,384,2048]{2,1,0:T(8,128)(2,1)}, u32[]{:S(2)}) copy-start(bf16[1,384,2048]{2,1,0:T(8,128)(2,1)} %param.11) | copy-start | bytes 4718596
  6.5 7.2 %copy-start.1 = (bf16[128,1024]{1,0:T(8,128)(2,1)S(1)}, bf16[128,1024]{1,0:T(8,128)(2,1)}, u32[]{:S(2)}) copy-start(bf16[128,1024]{1,0:T(8,128)(2,1)} %param.6) | copy-start | bytes 786436
  6.5 159.5 %all-gather.2.cloned.1.call-start = ((), (), s32[]{:S(2)}) async-start(), calls=%async_computation.3 | async-start | bytes 7864320 | tf_op jit(solution)/shard_map/all_gather | solution.py:40
  206.9 14.3 %copy-start.2 = (f32[128,8]{0,1:T(8,128)S(1)}, f32[128,8]{0,1:T(8,128)}, u32[]{:S(2)}) copy-start(f32[128,8]{0,1:T(8,128)} %param.7) | copy-start | bytes 12292
  206.9 110.6 %all-to-all-start.2 = ((bf16[128,10,1024]{2,1,0:T(8,128)(2,1)}), bf16[128,10,1024]{2,1,0:T(8,128)(2,1)}, u32[]{:S(2)}, u32[]{:S(2)}) async-start(bf16[128,10,1024]{2,1,0:T(8,128)(2,1)} %copy.31), calls=%async_computation.2 | async-start | bytes 8388608 | tf_op jit(solution)/shard_map/all_to_all | solution.py:50
Sparse Core Ops, SparseCore 0:
  149.0 16.9 all-gather.1
where the time goes:
time: 342 us
  blocking collectives  120 us (35%)
  waiting for transfers between devices  113 us (33%)
  local copies, waits for them, and re-layouts  51.4 us (15%)
  matrix products  19.2 us (6%)
  starting transfers between devices  14.3 us (4%)
  between operations  13.5 us (4%)
  other arithmetic  10.1 us (3%)
    all_to_all x1, blocking collectives, local(): lax.all_to_all(outgoing, 'ep', split_axis=0, concat_axis=0, tiled=True)  111 us
    all_to_all x1, waiting for transfers between devices, local(): lax.all_to_all(summed, 'ep', split_axis=0, concat_axis=0, tiled=True)  96.1 us
    all_gather x1, waiting for transfers between devices, local(): whole = lax.all_gather(received, 'half', axis=2, tiled=True)  17.1 us
    all_to_all x1, starting transfers between devices, local(): lax.all_to_all(summed, 'ep', split_axis=0, concat_axis=0, tiled=True)  14.3 us
    gather x2, local copies, waits for them, and re-layouts, local(): tokens[token_table] * filled[:, None]  11 us
    dot_general x1, matrix products, local(): jnp.einsum('secf,efd->secd', hidden, w_down, preferred_element_type=jnp.f...  9.81 us
    all_to_all x1, blocking collectives, summed_on_arrival(): blocks = lax.all_to_all(cut_along(value, dim, size), axis, 0, 0, tiled=True)  9.08 us
    gather x1, local copies, waits for them, and re-layouts, local(): answer.reshape(experts * capacity, -1)[slot].reshape(tok_dev, top, -1)  8.11 us
  transfers between devices with their start and end apart: 2, of which 2 were waited for; matrix products, arithmetic and copies ran while one was open for 0% of the time, Pallas kernels for 0%

commit v1 on v0

--- a/solution.py
+++ b/solution.py
@@ -1,7 +1,21 @@
+import functools
 import jax
 import jax.numpy as jnp
 from jax import lax
 from jax.sharding import PartitionSpec as P
+from jax.lax import all_to_all, axis_size
+
+
+def find_unit(values, comm_axis):
+    return jnp.concatenate(
+        all_to_all(
+            jnp.stack(axis_size(comm_axis) * [values]), comm_axis, split_axis=0, concat_axis=0
+        ),
+        axis=2,
+    )
+
+
+_edit_thing = functools.partial(find_unit, comm_axis="half")
 
 
 def cut_along(value, dim, size):
@@ -37,7 +51,7 @@
     outgoing = (tokens[token_table] * filled[:, None]).reshape(experts, capacity, half_width)
     received = lax.all_to_all(outgoing, "ep", split_axis=0, concat_axis=0, tiled=True)
     count = received.shape[1]
-    whole = lax.all_gather(received, "half", axis=2, tiled=True)
+    whole = _edit_thing(received)
     width = whole.shape[2]
     grouped = whole.reshape(-1, local_experts, count, width)
     gate = jnp.einsum("secd,edf->secf", grouped, w_gate, preferred_element_type=jnp.float32)

time: 342 us -> 314 us (0.918)
  waiting for transfers between devices: 113 us -> 96.1 us
  between operations: 13.5 us -> 0.18 us
  blocking collectives: 120 us -> 128 us
  starting transfers between devices: 14.3 us -> 9.41 us
    all_gather x1 -> x0, waiting for transfers between devices: 17.1 us -> none  [local(): whole = lax.all_gather(received, 'half', axis=2, tiled=True)]
    all_to_all x0 -> x1, blocking collectives: none -> 7.95 us  [find_unit(): all_to_all(jnp.stack(axis_size(comm_axis) * [values]), comm_axis, split_a...]
    all_to_all x1, starting transfers between devices: 14.3 us -> 9.41 us  [local(): lax.all_to_all(summed, 'ep', split_axis=0, concat_axis=0, tiled=True)]
  transfers between devices with their start and end apart: 2 -> 1, of which waited for: 2 -> 1; matrix products, arithmetic and copies ran while one was open for 0% -> 0% of each run, Pallas kernels for 0% -> 0%
where the time goes in v1:
time: 314 us
  blocking collectives  128 us (41%)
  waiting for transfers between devices  96.1 us (31%)
  local copies, waits for them, and re-layouts  53.2 us (17%)
  matrix products  16.2 us (5%)
  other arithmetic  10.6 us (3%)
  starting transfers between devices  9.41 us (3%)
    all_to_all x1, blocking collectives, local(): lax.all_to_all(outgoing, 'ep', split_axis=0, concat_axis=0, tiled=True)  111 us
    all_to_all x1, waiting for transfers between devices, local(): lax.all_to_all(summed, 'ep', split_axis=0, concat_axis=0, tiled=True)  96.1 us
    gather x2, local copies, waits for them, and re-layouts, local(): tokens[token_table] * filled[:, None]  11 us
    dot_general x1, matrix products, local(): jnp.einsum('secf,efd->secd', hidden, w_down, preferred_element_type=jnp.f...  9.8 us
    all_to_all x1, starting transfers between devices, local(): lax.all_to_all(summed, 'ep', split_axis=0, concat_axis=0, tiled=True)  9.41 us
    all_to_all x1, blocking collectives, summed_on_arrival(): blocks = lax.all_to_all(cut_along(value, dim, size), axis, 0, 0, tiled=True)  9.08 us
    gather x1, local copies, waits for them, and re-layouts, local(): answer.reshape(experts * capacity, -1)[slot].reshape(tok_dev, top, -1)  8.23 us
    all_to_all x1, blocking collectives, find_unit(): all_to_all(jnp.stack(axis_size(comm_axis) * [values]), comm_axis, split_a...  7.95 us
  transfers between devices with their start and end apart: 1, of which 1 were waited for; matrix products, arithmetic and copies ran while one was open for 0% of the time, Pallas kernels for 0%

profile of v1, /device:TPU:24, one launch (start us, length us, event | category | flops | bytes accessed | tf_op | source)
XLA Modules:
  0.0 313.5 jit_solution(3097670013584744453)
XLA Ops:
  0.0 0.9 copy.26
  1.1 0.7 broadcast_multiply_fusion.1
  2.9 4.3 %scatter_custom_fusion = s32[1280]{0:T(1024)S(1)} fusion(s32[1024]{0:T(1024)S(1)} %bitcast.95, s32[1024]{0:T(1024)S(1)} %add_select_fusion, s32[]{:T(128)} %constant.29.clone.1), kind=kCustom, calls=%fused_computation.43 | custom fusion | bytes 5124 | tf_op jit(solution)/shard_map/scatter | solution.py:45
  7.3 5.1 %gather_fusion = bf16[1280,1024]{1,0:T(8,128)(2,1)} fusion(bf16[128,1024]{1,0:T(8,128)(2,1)S(1)} %copy-done.2, s32[2048]{0:T(1024)S(1)} %pad_clamp_fusion), kind=kCustom, calls=%fused_computation | custom fusion | bytes 5248000 | tf_op jit(solution)/shard_map/gather | solution.py:51
  12.3 5.9 %gather.9 = bf16[128,10,1024]{2,1,0:T(8,128)(2,1)} reshape(bf16[1280,1024]{1,0:T(8,128)(2,1)} %gather_fusion) | data formatting | bytes 5242880 | tf_op jit(solution)/shard_map/gather | solution.py:51
  18.3 7.6 %scatter_custom_fusion.1 = bf16[1280]{0:T(1024)(128)(2,1)S(1)} fusion(s32[1024]{0:T(1024)S(1)} %bitcast.96, bf16[1024]{0:T(1024)(128)(2,1)S(1)} %broadcast.65, bf16[]{:T(256)} %constant.37.clone.1), kind=kCustom, calls=%fused_computation.47 | custom fusion | bytes 2562 | tf_op jit(solution)/shard_map/scatter | solution.py:49
  26.0 2.5 broadcast_multiply_fusion
  28.6 110.8 %all_to_all.20 = bf16[128,10,1024]{2,1,0:T(8,128)(2,1)S(1)} all-to-all(bf16[128,10,1024]{2,1,0:T(8,128)(2,1)S(1)} %broadcast_multiply_fusion), channel_id=1, replica_groups=mesh['ep'=128,'half'=2] {'ep'}, dimensions={0} | all-to-all | bytes 5242880 | tf_op jit(solution)/shard_map/all_to_all | solution.py:52
  139.4 1.4 copy.44
  141.3 7.9 %all_to_all.21 = bf16[2,128,10,1024]{3,1,2,0:T(8,128)(2,1)S(1)} all-to-all(bf16[2,128,10,1024]{3,1,2,0:T(8,128)(2,1)S(1)} %pad_maximum_fusion), channel_id=1, replica_groups=mesh['ep'=128,'half'=2] {'half'}, dimensions={0} | all-to-all | bytes 10485760 | tf_op jit(solution)/shard_map/all_to_all | solution.py:11
  149.3 0.9 copy.39
  150.1 2.3 copy-done.3
  152.4 4.1 %fusion.8 = f32[128,10,384]{2,0,1:T(8,128)} fusion(bf16[128,10,2048]{2,0,1:T(8,128)(2,1)S(1)} %bitcast.91, bf16[1,2048,384]{2,1,0:T(8,128)(2,1)S(1)} %copy-done.5), kind=kOutput, calls=%fused_computation.20 | convolution fusion | flops 2013265920 | bytes 8781824 | tf_op jit(solution)/shard_map/secd,edf->secf/dot_general | solution.py:57
  156.6 9.8 %convolution_convert_fusion = bf16[128,10,2048]{2,0,1:T(8,128)(2,1)} fusion(bf16[1,384,2048]{2,1,0:T(8,128)(2,1)S(1)} %copy-done, bf16[128,10,2048]{2,0,1:T(8,128)(2,1)} %bitcast.92, bf16[1,2048,384]{2,1,0:T(8,128)(2,1)} %param.10, f32[128,10,384]{2,0,1:T(8,128)} %fusion.8), kind=kOutput, calls=%fused_computation.6 | convolution fusion | flops 4032102400 | bytes 15597568 | tf_op jit(solution)/shard_map/secf,efd->secd/dot_general | solution.py:60
  166.4 3.3 %copy.43 = bf16[10,16,2,8,1024]{4,3,1,0,2:T(8,128)(2,1)S(1)} copy(bf16[10,16,2,8,1024]{4,3,2,1,0:T(8,128)(2,1)} %bitcast.93) | data formatting | bytes 10485760 | tf_op jit(solution)/shard_map/reshape | solution.py:23
  169.7 9.1 %all_to_all.22 = bf16[2,128,10,1024]{3,1,2,0:T(8,128)(2,1)} all-to-all(bf16[2,128,10,1024]{3,1,2,0:T(8,128)(2,1)S(1)} %bitcast.89), channel_id=1, replica_groups=mesh['ep'=128,'half'=2] {'half'}, dimensions={0} | all-to-all | bytes 10485760 | tf_op jit(solution)/shard_map/all_to_all | solution.py:29
  178.8 6.2 %reduce_sum.25 = bf16[128,10,1024]{2,0,1:T(8,128)(2,1)} reduce(bf16[2,128,10,1024]{3,1,2,0:T(8,128)(2,1)} %all_to_all.22, bf16[]{:T(256)} %constant.37.clone.1), dimensions={0}, to_apply=%region_5.6 | reduce | flops 1310720 | bytes 7864322 | tf_op jit(solution)/shard_map/reduce_sum | solution.py:30
  185.0 5.3 %copy.34 = bf16[128,10,1024]{2,1,0:T(8,128)(2,1)} copy(bf16[128,10,1024]{2,0,1:T(8,128)(2,1)} %reduce_sum.25) | data formatting | bytes 5242880 | tf_op jit(solution)/shard_map/reduce_sum | solution.py:30
  190.4 9.4 %all-to-all-start.3 = ((bf16[128,10,1024]{2,1,0:T(8,128)(2,1)}), bf16[128,10,1024]{2,1,0:T(8,128)(2,1)}, u32[]{:S(2)}, u32[]{:S(2)}) async-start(bf16[128,10,1024]{2,1,0:T(8,128)(2,1)} %copy.34), calls=%async_computation.3 | async-start | bytes 8388608 | tf_op jit(solution)/shard_map/all_to_all | solution.py:64
  200.0 96.1 %all-to-all-done.3 = bf16[128,10,1024]{2,1,0:T(8,128)(2,1)} async-done(((bf16[128,10,1024]{2,1,0:T(8,128)(2,1)}), bf16[128,10,1024]{2,1,0:T(8,128)(2,1)}, u32[]{:S(2)}, u32[]{:S(2)}) %all-to-all-start.3) | async-done | bytes 2621472 | tf_op jit(solution)/shard_map/all_to_all | solution.py:64
  296.1 6.1 %reshape.97 = bf16[1280,1024]{1,0:T(8,128)(2,1)} reshape(bf16[128,10,1024]{2,1,0:T(8,128)(2,1)} %all-to-all-done.3) | data formatting | bytes 5242880 | tf_op jit(solution)/shard_map/reshape | solution.py:65
  302.2 8.2 %gather_fusion.1 = bf16[1024,1024]{1,0:T(8,128)(2,1)} fusion(bf16[1280,1024]{1,0:T(8,128)(2,1)} %reshape.97, s32[1024]{0:T(1024)S(1)} %broadcast_clamp_fusion), kind=kCustom, calls=%fused_computation.1 | custom fusion | bytes 4198400 | tf_op jit(solution)/shard_map/gather | solution.py:65
  310.5 2.3 fusion
  312.8 0.8 copy.45
  (32 shorter events, 2.0 us)
Async XLA Ops:
  0.0 156.6 %copy-start = (bf16[1,384,2048]{2,1,0:T(8,128)(2,1)S(1)}, bf16[1,384,2048]{2,1,0:T(8,128)(2,1)}, u32[]{:S(2)}) copy-start(bf16[1,384,2048]{2,1,0:T(8,128)(2,1)} %param.11) | copy-start | bytes 4718596
  0.0 7.2 %copy-start.2 = (bf16[128,1024]{1,0:T(8,128)(2,1)S(1)}, bf16[128,1024]{1,0:T(8,128)(2,1)}, u32[]{:S(2)}) copy-start(bf16[128,1024]{1,0:T(8,128)(2,1)} %param.6) | copy-start | bytes 786436
  149.3 3.2 %copy-start.5 = (bf16[1,2048,384]{2,1,0:T(8,128)(2,1)S(1)}, bf16[1,2048,384]{2,1,0:T(8,128)(2,1)}, u32[]{:S(2)}) copy-start(bf16[1,2048,384]{2,1,0:T(8,128)(2,1)} %param.9) | copy-start | bytes 4718596
  150.1 2.3 copy-start.3
  190.4 9.4 %copy-start.4 = (f32[128,8]{0,1:T(8,128)S(1)}, f32[128,8]{0,1:T(8,128)}, u32[]{:S(2)}) copy-start(f32[128,8]{0,1:T(8,128)} %param.7) | copy-start | bytes 12292
  190.4 105.7 %all-to-all-start.3 = ((bf16[128,10,1024]{2,1,0:T(8,128)(2,1)}), bf16[128,10,1024]{2,1,0:T(8,128)(2,1)}, u32[]{:S(2)}, u32[]{:S(2)}) async-start(bf16[128,10,1024]{2,1,0:T(8,128)(2,1)} %copy.34), calls=%async_computation.3 | async-start | bytes 8388608 | tf_op jit(solution)/shard_map/all_to_all | solution.py:64
  302.2 11.3 %copy-start.1 = (bf16[1,384,2048]{2,1,0:T(8,128)(2,1)S(1)}, bf16[1,384,2048]{2,1,0:T(8,128)(2,1)}, u32[]{:S(2)}) copy-start(bf16[1,384,2048]{2,1,0:T(8,128)(2,1)} %param.11) | copy-start | bytes 4718596
